TPU v7x, 32 devices: a whole 2x2x4 slice. The times are simulated.
32 devices in a mesh: shard: 8 (over z, y), width: 4 (over x, core).
Axes of the slice: x: 2, y: 2, z: 4, core: 2. Of those that a mesh axis runs over, the one named last changes fastest.
Arguments:
- one_query: float32 [3584, 4096], P('shard', 'width'), may hold values from -0.125 to 0.125
- other_query: float32 [3584, 4096], P('shard', 'width'), may hold values from -0.09375 to 0.09375
- one_key: float32 [3584, 2048], P('shard', 'width'), may hold values from -0.125 to 0.125
- other_key: float32 [3584, 2048], P('shard', 'width'), may hold values from -0.09375 to 0.09375
- one_value: float32 [3584, 2048], P('shard', 'width'), may hold values from -0.125 to 0.125
- other_value: float32 [3584, 2048], P('shard', 'width'), may hold values from -0.09375 to 0.09375
- mix_share: float32 [3584], P('shard'), may hold values from 0.2 to 0.8
- norm_gain: float32 [3584], P('shard'), may hold values from 0.25 to 1.75
Outputs:
- final_query: bfloat16 [3584, 4096], P(None, 'width')
- final_key: bfloat16 [3584, 2048], P(None, 'width')
- final_value: bfloat16 [3584, 2048], P(None, 'width')
- scale_query: float32 [4096], P('width')
- scale_key: float32 [2048], P('width')
- scale_value: float32 [2048], P('width')
All inputs are finite; a program needn't handle non-finite values.
Results may differ from a plain program's by a relative error of at most 0.001.
Values may be sent and summed in bfloat16 or wider, within the bound.
A program may use at most 128 MiB of HBM per device.

v0:
```python
import functools

import jax
import jax.numpy as jnp
from jax import lax
from jax.experimental import pallas as pl
from jax.experimental.pallas import tpu as pltpu
from jax.sharding import PartitionSpec as P

MESH = pl.DeviceIdType.MESH
ROWS = 16
TILE = 8
LANES = 128
EARLY = ROWS


def plain(one_query, other_query, one_key, other_key, one_value, other_value, mix_share, norm_gain):
    result_query = mix_share[:, None] * one_query + (1.0 - mix_share[:, None]) * other_query
    result_key = mix_share[:, None] * one_key + (1.0 - mix_share[:, None]) * other_key
    result_value = mix_share[:, None] * one_value + (1.0 - mix_share[:, None]) * other_value
    result_gained_query = result_query * norm_gain[:, None]
    result_gained_key = result_key * norm_gain[:, None]
    result_gained_value = result_value * norm_gain[:, None]
    total_query, total_key, total_value = lax.psum(
        (
            jnp.sum(result_gained_query * result_gained_query, axis=0),
            jnp.sum(result_gained_key * result_gained_key, axis=0),
            jnp.sum(result_gained_value * result_gained_value, axis=0),
        ),
        "shard",
    )
    scale_query = jnp.sqrt(total_query)
    scale_key = jnp.sqrt(total_key)
    scale_value = jnp.sqrt(total_value)
    narrow_query, narrow_key, narrow_value = (
        (result_gained_query / scale_query).astype(jnp.bfloat16),
        (result_gained_key / scale_key).astype(jnp.bfloat16),
        (result_gained_value / scale_value).astype(jnp.bfloat16),
    )
    final_query, final_key, final_value = (
        lax.all_gather(narrow_query, "shard", axis=0, tiled=True),
        lax.all_gather(narrow_key, "shard", axis=0, tiled=True),
        lax.all_gather(narrow_value, "shard", axis=0, tiled=True),
    )
    return (final_query, final_key, final_value, scale_query, scale_key, scale_value)


def cuts(start, end, parts, unit):
    edges = [start + (end - start) // unit * part // parts * unit for part in range(parts)] + [end]
    return [(low, high - low) for low, high in zip(edges, edges[1:])]


def plan(rows, line):
    far = max(1, round(rows / (2 * (line - 1) * TILE))) * TILE
    pieces = [(0, EARLY)] + cuts(EARLY, rows - far, 2, ROWS)
    return pieces + [(rows - far, far)], len(pieces)


def gather_kernel(n, widths, share_ref, gain_ref, *refs):
    ins, (buf, scale_ref, first, second, left, right, sums, early, in_sem, sum_send, sum_recv, early_send, early_recv, send_sem, recv_sem) = refs[:6], refs[6:]
    rows = first.shape[0]
    total = sum(widths)
    line = n // 2
    me = lax.axis_index("shard")
    z, y = me // 2, me % 2
    other = z * 2 + 1 - y
    pieces, near = plan(rows, line)
    starts = [sum(widths[:i]) for i in range(len(widths))]

    loads = []
    parts = cuts(0, rows, 4, ROWS)
    for p, (low, size) in enumerate(parts):
        group = []
        for i, ref in enumerate(ins):
            dest = (first, second)[i % 2].at[pl.ds(low, size), pl.ds(starts[i // 2], widths[i // 2])]
            copy = pltpu.make_async_copy(ref.at[pl.ds(low, size), :], dest, in_sem.at[p, i])
            copy.start()
            group.append(copy)
        loads.append(group)

    barrier = pltpu.get_barrier_semaphore()
    for step in range(1, n):
        pl.semaphore_signal(barrier, inc=1, device_id={"shard": lax.rem(me + step, n)}, device_id_type=MESH)

    for low in range(0, rows, LANES):
        size = min(LANES, rows - low)
        share, gain = share_ref[:, low:low + size], gain_ref[:, low:low + size]
        for ref, row in ((left, share * gain), (right, (1.0 - share) * gain)):
            ref[pl.ds(low, size), :] = jnp.transpose(jnp.broadcast_to(row, (LANES, size)))

    def mixed(block, acc):
        at = pl.ds(pl.multiple_of(block * ROWS, ROWS), ROWS)
        ours, theirs = (jnp.concatenate([ref[at, :]] * 4, axis=1) for ref in (left, right))
        out = []
        for i in range(len(acc)):
            cols = pl.ds(i * 512, 512)
            value = ours * first[at, cols] + theirs * second[at, cols]
            first[at, cols] = value
            square = value * value
            out.append(acc[i] + square[:8] + square[8:])
        return tuple(out)

    acc = tuple(jnp.zeros((8, 512), jnp.float32) for _ in range(total // 512))
    for group, (low, size) in zip(loads, parts):
        for copy in group:
            copy.wait()
        acc = lax.fori_loop(low // ROWS, (low + size) // ROWS, mixed, acc)
    for i, value in enumerate(acc):
        sums[me, :, pl.ds(i * 512, 512)] = jnp.sum(value, axis=0, keepdims=True)

    pl.semaphore_wait(barrier, n - 1)

    def sum_copy(target, source):
        return pltpu.make_async_remote_copy(
            src_ref=sums.at[source], dst_ref=sums.at[source], send_sem=sum_send.at[target], recv_sem=sum_recv.at[source],
            device_id={"shard": target}, device_id_type=MESH)

    peers = [jnp.where(z < line // 2, line - 1 - k, k) * 2 + side for k in range(line) for side in (1 - y, y)]
    for peer in peers:
        @pl.when(peer != me)
        def _():
            sum_copy(peer, me).start()

    up, down, always = z < line - 1, z > 0, z >= 0
    targets = (jnp.minimum(z + 1, line - 1) * 2 + y, jnp.maximum(z - 1, 0) * 2 + y, other)

    def early_copy(way):
        return pltpu.make_async_remote_copy(
            src_ref=first.at[pl.ds(0, EARLY), :], dst_ref=early.at[way], send_sem=early_send.at[way],
            recv_sem=early_recv.at[way], device_id={"shard": targets[way]}, device_id_type=MESH)

    for way, condition in enumerate((up, down, always)):
        @pl.when(condition)
        def _():
            early_copy(way).start()

    for peer in peers:
        @pl.when(peer != me)
        def _():
            sum_copy(other, peer).wait_recv()
    whole = sums[0]
    for source in range(1, n):
        whole = whole + sums[source]
    scale = jnp.sqrt(whole)
    scale_ref[...] = scale
    inverse = jnp.broadcast_to(1.0 / scale, (8, total))

    def copy(way, source, c):
        low, size = pieces[c]
        ref = buf.at[source, pl.ds(low, size), :]
        return pltpu.make_async_remote_copy(
            src_ref=ref, dst_ref=ref, send_sem=send_sem.at[way, source, c], recv_sem=recv_sem.at[source, c],
            device_id={"shard": targets[way]}, device_id_type=MESH)

    sent = []

    def scaled(source, ref):
        def step(block, carry):
            at = pl.ds(pl.multiple_of(block * ROWS, ROWS), ROWS)
            for i in range(total // 512):
                cols = pl.ds(i * 512, 512)
                wide = jnp.concatenate([inverse[:, i * 512:(i + 1) * 512]] * 2, axis=0)
                buf[source, at, cols] = (ref[at, cols] * wide).astype(buf.dtype)
            return carry
        return step

    def issue(condition, way, source, c):
        @pl.when(condition)
        def _():
            copy(way, source, c).start()
        sent.append((condition, way, source, c))

    def issue_own(c):
        issue(up, 0, me, c)
        issue(down, 1, me, c)
        issue(always, 2, me, c)

    done = 0
    for c, (low, size) in enumerate(pieces):
        lax.fori_loop(done, pl.cdiv(low + size, ROWS), scaled(me, first), 0)
        done = pl.cdiv(low + size, ROWS)
        if c > 1:
            issue_own(c - 1)
    issue_own(len(pieces) - 1)

    for way, (condition, source) in enumerate(((down, me - 2), (up, me + 2), (always, other))):
        @pl.when(condition)
        def _():
            early_copy(way).wait_recv()
            lax.fori_loop(0, EARLY // ROWS, scaled(source, early.at[way]), 0)
    issue(down & up, 0, me - 2, 0)
    issue(down, 2, me - 2, 0)
    issue(up & down, 1, me + 2, 0)
    issue(up, 2, me + 2, 0)

    def pass_on(condition, source, c, ways):
        @pl.when(condition)
        def _():
            copy(2, source, c).wait_recv()
        for extra, way in ways:
            issue(condition & extra, way, source, c)

    def relay(step):
        for c in range(near, len(pieces)):
            if step == 0:
                pass_on(always, other, c, [(up, 0), (down, 1)])
            else:
                pass_on(z >= step, other - 2 * step, c, [(up, 0)])
                pass_on(z + step < line, other + 2 * step, c, [(down, 1)])

    for step in range(1, line):
        for c in range(1 if step == 1 else 0, len(pieces)):
            across = [(always, 2)] if c < near else []
            pass_on(z >= step, me - 2 * step, c, [(up, 0)] + across)
            pass_on(z + step < line, me + 2 * step, c, [(down, 1)] + across)
        relay(step - 1)
    relay(line - 1)
    for c in range(1, near):
        pass_on(always, other, c, [])
    for step in range(1, line):
        for c in range(near):
            pass_on(z >= step, other - 2 * step, c, [])
            pass_on(z + step < line, other + 2 * step, c, [])
    for condition, way, source, c in sent:
        @pl.when(condition)
        def _():
            copy(way, source, c).wait_send()
    for way, condition in enumerate((up, down, always)):
        @pl.when(condition)
        def _():
            early_copy(way).wait_send()
    for peer in peers:
        @pl.when(peer != me)
        def _():
            sum_copy(peer, me).wait_send()


def store_kernel(n, widths, buf, scale_ref, *refs):
    outs, scales, sem = refs[:3], refs[3:6], refs[6]
    rows = buf.shape[1]
    copies = []
    for source in range(n):
        start = 0
        for i, width in enumerate(widths):
            copies.append(pltpu.make_async_copy(
                buf.at[source, :, pl.ds(start, width)], outs[i].at[pl.ds(source * rows, rows), :], sem.at[source, i]))
            copies[-1].start()
            start += width
    start = 0
    for i, width in enumerate(widths):
        scales[i][...] = scale_ref[:, start:start + width]
        start += width
    for copy in copies:
        copy.wait()


def routed(n, one_query, other_query, one_key, other_key, one_value, other_value, mix_share, norm_gain):
    widths = (one_query.shape[1], one_key.shape[1], one_value.shape[1])
    rows, total = one_query.shape[0], sum(widths)
    pieces = len(plan(rows, n // 2)[0])
    vmem = pl.BlockSpec(memory_space=pltpu.VMEM)
    hbm = pl.BlockSpec(memory_space=pl.ANY)
    buf, scale = pl.pallas_call(
        functools.partial(gather_kernel, n, widths),
        out_shape=(pltpu.VMEM((n, rows, total), jnp.bfloat16), pltpu.VMEM((1, total), jnp.float32)),
        in_specs=[vmem] * 2 + [hbm] * 6,
        out_specs=(vmem, vmem),
        scratch_shapes=[
            pltpu.VMEM((rows, total), jnp.float32),
            pltpu.VMEM((rows, total), jnp.float32),
            pltpu.VMEM((rows, LANES), jnp.float32),
            pltpu.VMEM((rows, LANES), jnp.float32),
            pltpu.VMEM((n, 1, total), jnp.float32),
            pltpu.VMEM((3, EARLY, total), jnp.float32),
            pltpu.SemaphoreType.DMA((4, 6)),
            pltpu.SemaphoreType.DMA((n,)),
            pltpu.SemaphoreType.DMA((n,)),
            pltpu.SemaphoreType.DMA((3,)),
            pltpu.SemaphoreType.DMA((3,)),
            pltpu.SemaphoreType.DMA((3, n, pieces)),
            pltpu.SemaphoreType.DMA((n, pieces)),
        ],
        compiler_params=pltpu.CompilerParams(collective_id=0, has_side_effects=True, vmem_limit_bytes=44 * 2**20),
    )(mix_share[None, :], norm_gain[None, :], one_query, other_query, one_key, other_key, one_value, other_value)
    outs = pl.pallas_call(
        functools.partial(store_kernel, n, widths),
        out_shape=tuple(jax.ShapeDtypeStruct((n * rows, width), jnp.bfloat16) for width in widths)
        + tuple(jax.ShapeDtypeStruct((1, width), jnp.float32) for width in widths),
        in_specs=[vmem, vmem],
        out_specs=(hbm,) * 3 + (vmem,) * 3,
        scratch_shapes=[pltpu.SemaphoreType.DMA((n, 3))],
        compiler_params=pltpu.CompilerParams(vmem_limit_bytes=2**20),
    )(pltpu.with_memory_space_constraint(buf, pltpu.VMEM), pltpu.with_memory_space_constraint(scale, pltpu.VMEM))
    return outs[:3] + tuple(out[0] for out in outs[3:])


def solution(mesh):
    n = mesh.shape["shard"]

    def body(*args):
        if n % 2 or n < 4 or args[0].shape[0] % ROWS or args[0].shape[0] < 6 * ROWS:
            return plain(*args)
        return routed(n, *args)

    return jax.shard_map(
        body,
        mesh=mesh,
        in_specs=(
            P("shard", "width"),
            P("shard", "width"),
            P("shard", "width"),
            P("shard", "width"),
            P("shard", "width"),
            P("shard", "width"),
            P("shard"),
            P("shard"),
        ),
        out_specs=(
            P(None, "width"),
            P(None, "width"),
            P(None, "width"),
            P("width"),
            P("width"),
            P("width"),
        ),
        check_vma=False,
    )
```

profile of v0, /device:TPU:0, one launch (start us, length us, event | category | flops | bytes accessed | tf_op | source)
XLA Modules:
  0.0 157.8 jit_solution(9271417218500321119)
XLA Ops:
  0.6 151.2 %shard_map.127 = (bf16[8,448,2048]{2,1,0:T(8,128)(2,1)S(1)}, f32[1,2048]{1,0:T(1,128)S(1)}) custom-call(f32[1,448]{1,0:T(1,128)} %bitcast.5, f32[1,448]{1,0:T(1,128)} %bitcast.6, f32[448,1024]{1,0:T(8,128)} %refs_0_.1, f32[448,1024]{1,0:T(8,128)} %refs_1_.1, f32[448,512]{1,0:T(8,128)} %refs_2_.1, f32[448,512]{1,0:T(8,128)} %refs_3_.1, f32[448,512]{1,0:T(8,128)} %refs_4_.1, ...), custom_call_target="tpu_custom_call" | custom-call | tf_op jit(solution)/shard_map/pallas_call | solution.py:263
  151.8 6.0 %shard_map.128 = (bf16[3584,1024]{1,0:T(8,128)(2,1)}, bf16[3584,512]{1,0:T(8,128)(2,1)}, bf16[3584,512]{1,0:T(8,128)(2,1)}, f32[1,1024]{1,0:T(1,128)}, f32[1,512]{1,0:T(1,128)}, /*index=5*/f32[1,512]{1,0:T(1,128)}) custom-call(bf16[8,448,2048]{2,1,0:T(8,128)(2,1)S(1)} %get-tuple-element.14.buf, f32[1,2048]{1,0:T(1,128)S(1)} %get-tuple-element.15.scale_ref), custom_call_target="tpu_custom_call" | custom-call | tf_op jit(solution)/shard_map/pallas_call | solution.py:285
where the time goes:
time: 158 us
  Pallas kernels  157 us (99%)
    pallas_call x1, Pallas kernels, routed(): pl.pallas_call(functools.partial(gather_kernel, n, widths), out_shape=(pl...  151 us
    pallas_call x1, Pallas kernels, routed(): pl.pallas_call(functools.partial(store_kernel, n, widths), out_shape=tupl...  5.98 us

commit v1 on v0

v1 whole, which is shorter than its diff:
```python
import functools
import heapq

import jax
import jax.numpy as jnp
from jax import lax
from jax.experimental import pallas as pl
from jax.experimental.pallas import tpu as pltpu
from jax.sharding import PartitionSpec as P

MESH = pl.DeviceIdType.MESH
ROWS = 16
TILE = 8
LANES = 128
EARLY = (8, 24)
UP, DOWN, ACROSS = range(3)
PARTS = 3


def plain(one_query, other_query, one_key, other_key, one_value, other_value, mix_share, norm_gain):
    result_query = mix_share[:, None] * one_query + (1.0 - mix_share[:, None]) * other_query
    result_key = mix_share[:, None] * one_key + (1.0 - mix_share[:, None]) * other_key
    result_value = mix_share[:, None] * one_value + (1.0 - mix_share[:, None]) * other_value
    result_gained_query = result_query * norm_gain[:, None]
    result_gained_key = result_key * norm_gain[:, None]
    result_gained_value = result_value * norm_gain[:, None]
    total_query, total_key, total_value = lax.psum(
        (
            jnp.sum(result_gained_query * result_gained_query, axis=0),
            jnp.sum(result_gained_key * result_gained_key, axis=0),
            jnp.sum(result_gained_value * result_gained_value, axis=0),
        ),
        "shard",
    )
    scale_query = jnp.sqrt(total_query)
    scale_key = jnp.sqrt(total_key)
    scale_value = jnp.sqrt(total_value)
    narrow_query, narrow_key, narrow_value = (
        (result_gained_query / scale_query).astype(jnp.bfloat16),
        (result_gained_key / scale_key).astype(jnp.bfloat16),
        (result_gained_value / scale_value).astype(jnp.bfloat16),
    )
    final_query, final_key, final_value = (
        lax.all_gather(narrow_query, "shard", axis=0, tiled=True),
        lax.all_gather(narrow_key, "shard", axis=0, tiled=True),
        lax.all_gather(narrow_value, "shard", axis=0, tiled=True),
    )
    return (final_query, final_key, final_value, scale_query, scale_key, scale_value)


def cuts(start, end, parts, unit):
    edges = [start + (end - start) // unit * part // parts * unit for part in range(parts)] + [end]
    return [(low, high - low) for low, high in zip(edges, edges[1:])]


def plan(rows):
    early = sum(EARLY)
    half = rows // 2 // ROWS * ROWS
    near = [(0, early)] + cuts(early, half, 2, ROWS)
    return near + [(half, rows - half)], len(near)


def sending(level, line, pieces, order):
    own = sum(size for _, size in pieces[1:])
    sent = [own if ok else 0 for ok in (level < line - 1, level > 0, True)]
    for _, _, c, ways, _ in order[level]:
        for way in ways:
            sent[way] += pieces[c][1]
    return sent


def folded(amount, rows, n):
    return next((d for d in range(1, n + 1) if amount % (d * TILE) == 0 and amount // d <= rows), None)


def fits(n, rows):
    if n % 2 or n < 4 or rows % ROWS or rows < 4 * sum(EARLY):
        return False
    pieces, near = plan(rows)
    order = relays(n // 2, pieces, near)
    return all(not amount or folded(amount, rows, n) for z in range(n // 2) for amount in sending(z, n // 2, pieces, order))


def stages(rows, lead):
    return [(0, lead)] + cuts(lead, rows, PARTS, ROWS)


def relays(line, pieces, near):
    latency = 3 * TILE
    events, free, order = [], {}, [[] for _ in range(line)]

    def send(time, z, way, column, source, c):
        start = max(time, free.get((z, way), 0))
        free[z, way] = start + pieces[c][1]
        target = (z + 1, z - 1, z)[way]
        heapq.heappush(events, (free[z, way] + latency, len(events), target, column ^ (way == ACROSS), source, c))

    def onward(z, column, source, c):
        along = [UP] if (source < z or source == z == 0) and z < line - 1 else []
        along += [DOWN] if (source > z or source == z == line - 1) and z > 0 else []
        crosses = source not in (0, line - 1) or c < near
        if column == 0:
            return along + ([ACROSS] if crosses else [])
        return [] if crosses else along

    for z in range(line):
        for c in range(1, len(pieces)):
            for way, ok in ((UP, z < line - 1), (DOWN, z > 0), (ACROSS, True)):
                if ok:
                    send(0, z, way, 0, z, c)
        for way, ok in ((UP, z < line - 1), (DOWN, z > 0), (ACROSS, True)):
            if ok:
                target = (z + 1, z - 1, z)[way]
                heapq.heappush(events, (0, len(events), target, int(way == ACROSS), z, 0))
    serial = 0
    while events:
        time, _, z, column, source, c = heapq.heappop(events)
        ways = onward(z, column, source, c)
        direct = c == 0 and (abs(source - z) == 1 and column == 0 or source == z)
        order[z].append((column, source, c, ways, direct))
        for way in ways:
            start = max(time, free.get((z, way), 0))
            free[z, way] = start + pieces[c][1]
            serial += 1
            heapq.heappush(events, (free[z, way] + latency, 10**6 + serial, (z + 1, z - 1, z)[way], column ^ (way == ACROSS), source, c))
    return order


def gather_kernel(n, widths, *refs):
    (share_hbm, gain_hbm), ins, (buf, scale_ref, share_ref, gain_ref, first, second, left, right, sums, early, row_sem, in_sem, sum_sem, early_send, early_recv, send_sem, recv_sem) = refs[:2], refs[2:8], refs[8:]
    rows = first.shape[0]
    total = sum(widths)
    line = n // 2
    me = lax.axis_index("shard")
    z, y = me // 2, me % 2
    other = z * 2 + 1 - y
    pieces, near = plan(rows)
    order = relays(line, pieces, near)
    lead = sum(EARLY)
    starts = [sum(widths[:i]) for i in range(len(widths))]

    vectors = [
        pltpu.make_async_copy(source, dest, row_sem.at[i])
        for i, (source, dest) in enumerate(((share_hbm, share_ref), (gain_hbm, gain_ref)))
    ]
    for copy in vectors:
        copy.start()
    loads = []
    parts = stages(rows, lead)
    for p, (low, size) in enumerate(parts):
        for i, ref in enumerate(ins):
            dest = (first, second)[i % 2].at[pl.ds(low, size), pl.ds(starts[i // 2], widths[i // 2])]
            pltpu.make_async_copy(ref.at[pl.ds(low, size), :], dest, in_sem.at[p, i % 2]).start()
        whole = [ref.at[pl.ds(low, size), :] for ref in (first, second)]
        loads.append([pltpu.make_async_copy(ref, ref, in_sem.at[p, i]) for i, ref in enumerate(whole)])

    barrier = pltpu.get_barrier_semaphore()
    for step in range(1, n):
        pl.semaphore_signal(barrier, inc=1, device_id={"shard": lax.rem(me + step, n)}, device_id_type=MESH)

    for copy in vectors:
        copy.wait()
    for low in range(0, rows, LANES):
        size = min(LANES, rows - low)
        share, gain = share_ref[:, low:low + size], gain_ref[:, low:low + size]
        for ref, row in ((left, share * gain), (right, (1.0 - share) * gain)):
            ref[pl.ds(low, size), :] = jnp.transpose(jnp.broadcast_to(row, (LANES, size)))

    def mixed(block, acc):
        at = pl.ds(pl.multiple_of(block * ROWS, ROWS), ROWS)
        ours, theirs = (jnp.concatenate([ref[at, :]] * 4, axis=1) for ref in (left, right))
        out = []
        for i in range(len(acc)):
            cols = pl.ds(i * 512, 512)
            value = ours * first[at, cols] + theirs * second[at, cols]
            first[at, cols] = value
            square = value * value
            out.append(acc[i] + square[:8] + square[8:])
        return tuple(out)

    up, down, always = z < line - 1, z > 0, z >= 0
    conditions = (up, down, always)
    targets = (jnp.minimum(z + 1, line - 1) * 2 + y, jnp.maximum(z - 1, 0) * 2 + y, other)

    def early_copy(way, low, size):
        return pltpu.make_async_remote_copy(
            src_ref=first.at[pl.ds(low, size), :], dst_ref=early.at[way, pl.ds(low, size), :],
            send_sem=early_send.at[way], recv_sem=early_recv.at[way],
            device_id={"shard": targets[way]}, device_id_type=MESH)

    def start_early(k):
        for way, condition in enumerate(conditions):
            @pl.when(condition)
            def _():
                early_copy(way, sum(EARLY[:k]), EARLY[k]).start()

    acc = tuple(jnp.zeros((8, 512), jnp.float32) for _ in range(total // 512))
    for p, (group, (low, size)) in enumerate(zip(loads, parts)):
        for copy in group:
            copy.wait()
        acc = lax.fori_loop(low // ROWS, (low + size) // ROWS, mixed, acc)
        if p == 1:
            pl.semaphore_wait(barrier, n - 1)
            start_early(0)
    for i, value in enumerate(acc):
        sums[me, :, pl.ds(i * 512, 512)] = jnp.sum(value, axis=0, keepdims=True)

    def sum_copy(target, ref):
        return pltpu.make_async_remote_copy(
            src_ref=ref, dst_ref=ref, send_sem=sum_sem.at[0], recv_sem=sum_sem.at[1],
            device_id={"shard": target}, device_id_type=MESH)

    peers = [jnp.where(z < line // 2, line - 1 - k, k) * 2 + side for k in range(line) for side in (1 - y, y)]
    for peer in peers:
        @pl.when(peer != me)
        def _():
            sum_copy(peer, sums.at[me]).start()
    for k in range(1, len(EARLY)):
        start_early(k)

    everyone = sum_copy(other, sums.at[pl.ds(0, n - 1)])
    everyone.wait_recv()
    whole = sums[0]
    for source in range(1, n):
        whole = whole + sums[source]
    scale = jnp.sqrt(whole)
    scale_ref[...] = scale
    inverse = jnp.broadcast_to(1.0 / scale, (8, total))

    def scaled(source, ref):
        def step(block, carry):
            at = pl.ds(pl.multiple_of(block * ROWS, ROWS), ROWS)
            for i in range(total // 512):
                cols = pl.ds(i * 512, 512)
                wide = jnp.concatenate([inverse[:, i * 512:(i + 1) * 512]] * 2, axis=0)
                buf[source, at, cols] = (ref[at, cols] * wide).astype(buf.dtype)
            return carry
        return step

    def copy(way, source, c):
        low, size = pieces[c]
        ref = buf.at[source, pl.ds(low, size), :]
        return pltpu.make_async_remote_copy(
            src_ref=ref, dst_ref=ref, send_sem=send_sem.at[way], recv_sem=recv_sem.at[source, c],
            device_id={"shard": targets[way]}, device_id_type=MESH)

    def issue_own(c):
        for way, condition in enumerate(conditions):
            @pl.when(condition)
            def _():
                copy(way, me, c).start()

    for c, (low, size) in enumerate(pieces[1:], 1):
        lax.fori_loop(low // ROWS, (low + size) // ROWS, scaled(me, first), 0)
        if c == 1:
            lax.fori_loop(0, lead // ROWS, scaled(me, first), 0)
            issue_own(c)
        if c > 2:
            issue_own(c - 1)
    issue_own(len(pieces) - 1)

    for way, (condition, source) in enumerate(((down, me - 2), (up, me + 2), (always, other))):
        @pl.when(condition)
        def _():
            early_copy(way, 0, lead).wait_recv()
            lax.fori_loop(0, lead // ROWS, scaled(source, early.at[way]), 0)

    for level in range(line):
        @pl.when(z == level)
        def _():
            for column, at, c, ways, direct in order[level]:
                source = at * 2 + (1 - y if column else y)
                if not direct:
                    copy(ACROSS, source, c).wait_recv()
                for way in ways:
                    copy(way, source, c).start()
            for way, amount in enumerate(sending(level, line, pieces, order)):
                if amount:
                    depth = folded(amount, rows, n)
                    ref = buf.at[pl.ds(0, depth), pl.ds(0, amount // depth), :]
                    pltpu.make_async_remote_copy(
                        src_ref=ref, dst_ref=ref, send_sem=send_sem.at[way], recv_sem=recv_sem.at[0, 0],
                        device_id={"shard": targets[way]}, device_id_type=MESH).wait_send()

    for way, condition in enumerate(conditions):
        @pl.when(condition)
        def _():
            early_copy(way, 0, lead).wait_send()
    everyone.wait_send()


def store_kernel(widths, buf, scale_ref, *refs):
    outs, scales, sem = refs[:3], refs[3:6], refs[6]
    copies = []
    start = 0
    for i, width in enumerate(widths):
        copies.append(pltpu.make_async_copy(buf.at[:, :, pl.ds(start, width)], outs[i], sem.at[0, i]))
        copies.append(pltpu.make_async_copy(scale_ref.at[:, pl.ds(start, width)], scales[i], sem.at[1, i]))
        start += width
    for copy in copies:
        copy.start()
    for copy in copies:
        copy.wait()


def routed(n, one_query, other_query, one_key, other_key, one_value, other_value, mix_share, norm_gain):
    widths = (one_query.shape[1], one_key.shape[1], one_value.shape[1])
    rows, total = one_query.shape[0], sum(widths)
    pieces = len(plan(rows)[0])
    lead = sum(EARLY)
    vmem = pl.BlockSpec(memory_space=pltpu.VMEM)
    hbm = pl.BlockSpec(memory_space=pl.ANY)
    buf, scale = pl.pallas_call(
        functools.partial(gather_kernel, n, widths),
        out_shape=(pltpu.VMEM((n, rows, total), jnp.bfloat16), pltpu.VMEM((1, total), jnp.float32)),
        in_specs=[hbm] * 8,
        out_specs=(vmem, vmem),
        scratch_shapes=[
            pltpu.VMEM((1, rows), jnp.float32),
            pltpu.VMEM((1, rows), jnp.float32),
            pltpu.VMEM((rows, total), jnp.float32),
            pltpu.VMEM((rows, total), jnp.float32),
            pltpu.VMEM((rows, LANES), jnp.float32),
            pltpu.VMEM((rows, LANES), jnp.float32),
            pltpu.VMEM((n, 1, total), jnp.float32),
            pltpu.VMEM((3, lead, total), jnp.float32),
            pltpu.SemaphoreType.DMA((2,)),
            pltpu.SemaphoreType.DMA((PARTS + 1, 2)),
            pltpu.SemaphoreType.DMA((2,)),
            pltpu.SemaphoreType.DMA((3,)),
            pltpu.SemaphoreType.DMA((3,)),
            pltpu.SemaphoreType.DMA((3,)),
            pltpu.SemaphoreType.DMA((n, pieces)),
        ],
        compiler_params=pltpu.CompilerParams(collective_id=0, has_side_effects=True, vmem_limit_bytes=44 * 2**20),
    )(mix_share[None, :], norm_gain[None, :], one_query, other_query, one_key, other_key, one_value, other_value)
    outs = pl.pallas_call(
        functools.partial(store_kernel, widths),
        out_shape=tuple(jax.ShapeDtypeStruct((n, rows, width), jnp.bfloat16) for width in widths)
        + tuple(jax.ShapeDtypeStruct((1, width), jnp.float32) for width in widths),
        in_specs=[vmem, vmem],
        out_specs=(hbm,) * 6,
        scratch_shapes=[pltpu.SemaphoreType.DMA((2, 3))],
        compiler_params=pltpu.CompilerParams(vmem_limit_bytes=2**20),
    )(pltpu.with_memory_space_constraint(buf, pltpu.VMEM), pltpu.with_memory_space_constraint(scale, pltpu.VMEM))
    return tuple(out.reshape(n * rows, -1) for out in outs[:3]) + tuple(out[0] for out in outs[3:])


def solution(mesh):
    n = mesh.shape["shard"]

    def body(*args):
        return routed(n, *args) if fits(n, args[0].shape[0]) else plain(*args)

    return jax.shard_map(
        body,
        mesh=mesh,
        in_specs=(
            P("shard", "width"),
            P("shard", "width"),
            P("shard", "width"),
            P("shard", "width"),
            P("shard", "width"),
            P("shard", "width"),
            P("shard"),
            P("shard"),
        ),
        out_specs=(
            P(None, "width"),
            P(None, "width"),
            P(None, "width"),
            P("width"),
            P("width"),
            P("width"),
        ),
        check_vma=False,
    )
```

time: 158 us -> 155 us (0.981)
  Pallas kernels: 157 us -> 154 us
    pallas_call x1, Pallas kernels: 151 us -> 149 us  [routed(): pl.pallas_call(functools.partial(gather_kernel, n, widths), out_shape=(pl...]
where the time goes in v1:
time: 155 us
  Pallas kernels  154 us (99%)
    pallas_call x1, Pallas kernels, routed(): pl.pallas_call(functools.partial(gather_kernel, n, widths), out_shape=(pl...  149 us
    pallas_call x1, Pallas kernels, routed(): pl.pallas_call(functools.partial(store_kernel, widths), out_shape=tuple((...  5.42 us

profile of v1, /device:TPU:0, one launch (start us, length us, event | category | flops | bytes accessed | tf_op | source)
XLA Modules:
  0.0 155.1 jit_solution(4661912718876374460)
XLA Ops:
  0.6 149.1 %shard_map.127 = (bf16[8,448,2048]{2,1,0:T(8,128)(2,1)S(1)}, f32[1,2048]{1,0:T(1,128)S(1)}) custom-call(f32[1,448]{1,0:T(1,128)} %bitcast.8, f32[1,448]{1,0:T(1,128)} %bitcast.9, f32[448,1024]{1,0:T(8,128)} %refs_2_.1, f32[448,1024]{1,0:T(8,128)} %refs_3_.1, f32[448,512]{1,0:T(8,128)} %refs_4_.1, f32[448,512]{1,0:T(8,128)} %refs_5_.1, f32[448,512]{1,0:T(8,128)} %refs_6_.1, ...), custom_call_target="tpu_custom_call" | custom-call | tf_op jit(solution)/shard_map/pallas_call | solution.py:313
  149.7 5.4 %shard_map.128 = (bf16[8,448,1024]{2,1,0:T(8,128)(2,1)}, bf16[8,448,512]{2,1,0:T(8,128)(2,1)}, bf16[8,448,512]{2,1,0:T(8,128)(2,1)}, f32[1,1024]{1,0:T(1,128)}, f32[1,512]{1,0:T(1,128)}, /*index=5*/f32[1,512]{1,0:T(1,128)}) custom-call(bf16[8,448,2048]{2,1,0:T(8,128)(2,1)S(1)} %get-tuple-element.14.buf, f32[1,2048]{1,0:T(1,128)S(1)} %get-tuple-element.15.scale_ref), custom_call_target="tpu_custom_call" | custom-call | tf_op jit(solution)/shard_map/pallas_call | solution.py:337

commit v2 on v1

v2 whole, which is shorter than its diff:
```python
import functools
import heapq

import jax
import jax.numpy as jnp
from jax import lax
from jax.experimental import pallas as pl
from jax.experimental.pallas import tpu as pltpu
from jax.sharding import PartitionSpec as P

MESH = pl.DeviceIdType.MESH
ROWS = 16
TILE = 8
LANES = 128
FIRST = ((16, 16, 16, 0), (8, 8, 16, 0))
LEADS = ((48, 48, 32, 32), (16, 16, 16, 16))
UP, DOWN, ACROSS = range(3)
PARTS = 5
FLIGHT = 3
MOST = max(map(max, LEADS))
START = 0


def plain(one_query, other_query, one_key, other_key, one_value, other_value, mix_share, norm_gain):
    result_query = mix_share[:, None] * one_query + (1.0 - mix_share[:, None]) * other_query
    result_key = mix_share[:, None] * one_key + (1.0 - mix_share[:, None]) * other_key
    result_value = mix_share[:, None] * one_value + (1.0 - mix_share[:, None]) * other_value
    result_gained_query = result_query * norm_gain[:, None]
    result_gained_key = result_key * norm_gain[:, None]
    result_gained_value = result_value * norm_gain[:, None]
    total_query, total_key, total_value = lax.psum(
        (
            jnp.sum(result_gained_query * result_gained_query, axis=0),
            jnp.sum(result_gained_key * result_gained_key, axis=0),
            jnp.sum(result_gained_value * result_gained_value, axis=0),
        ),
        "shard",
    )
    scale_query = jnp.sqrt(total_query)
    scale_key = jnp.sqrt(total_key)
    scale_value = jnp.sqrt(total_value)
    narrow_query, narrow_key, narrow_value = (
        (result_gained_query / scale_query).astype(jnp.bfloat16),
        (result_gained_key / scale_key).astype(jnp.bfloat16),
        (result_gained_value / scale_value).astype(jnp.bfloat16),
    )
    final_query, final_key, final_value = (
        lax.all_gather(narrow_query, "shard", axis=0, tiled=True),
        lax.all_gather(narrow_key, "shard", axis=0, tiled=True),
        lax.all_gather(narrow_value, "shard", axis=0, tiled=True),
    )
    return (final_query, final_key, final_value, scale_query, scale_key, scale_value)


def cuts(start, end, parts, unit):
    edges = [start + (end - start) // unit * part // parts * unit for part in range(parts)] + [end]
    return [(low, high - low) for low, high in zip(edges, edges[1:])]


def table(values, z, line):
    return values[z] if z < 2 else values[max(z - line, -2)]


def plan(rows, line, core):
    half = rows // 2 // ROWS * ROWS
    leads = [table(LEADS[core], z, line) for z in range(line)]
    return [[(0, lead)] + cuts(lead, half, 2, ROWS) + [(half, rows - half)] for lead in leads]


def ways_from(z, line):
    return [way for way, ok in ((UP, z < line - 1), (DOWN, z > 0), (ACROSS, True)) if ok]


def early_from(z, line):
    return [way for way, ok in ((UP, z == line - 2), (DOWN, z == 1), (ACROSS, z in (0, line - 1))) if ok]


def relays(line, pieces):
    latency = 3 * TILE
    events, free, serial, order = [], {}, [], [[] for _ in range(line)]

    def send(time, z, way, column, source, c, early=False):
        target = (z + 1, z - 1, z)[way]
        if not early:
            time = free[z, way] = max(time, free.get((z, way), 0)) + pieces[source][c][1]
        serial.append(None)
        heapq.heappush(events, (time + latency * (not early), len(serial), target, column ^ (way == ACROSS), source, c, early))

    def onward(z, column, source, c):
        along = [UP] if (source < z or source == z == 0) and z < line - 1 else []
        along += [DOWN] if (source > z or source == z == line - 1) and z > 0 else []
        crosses = source not in (0, line - 1) or c < len(pieces[source]) - 1
        if column == 0:
            return along + ([ACROSS] if crosses else [])
        return [] if crosses else along

    for z in range(line):
        for way in ways_from(z, line):
            for c in range(len(pieces[z])):
                send(0, z, way, 0, z, c, c == 0 and way in early_from(z, line))
    while events:
        time, _, z, column, source, c, early = heapq.heappop(events)
        ways = onward(z, column, source, c)
        order[z].append((column, source, c, ways, early))
        for way in ways:
            send(time, z, way, column, source, c)
    return order


def sending(level, line, pieces, order):
    early, leaving = early_from(level, line), ways_from(level, line)
    sent = [[sum(size for _, size in pieces[level][way in early:]) if way in leaving else 0, 0] for way in range(3)]
    for _, source, c, ways, _ in order[level]:
        for way in ways:
            sent[way][1] += pieces[source][c][1]
    return sent


def folded(amount, rows, n):
    return next((d for d in range(1, n + 1) if amount % (d * TILE) == 0 and amount // d <= rows), None)


def fits(n, rows):
    if n % 2 or n < 8 or rows % ROWS or rows < 4 * MOST:
        return False
    line = n // 2
    plans = [plan(rows, line, core) for core in range(2)]
    orders = [relays(line, pieces) for pieces in plans]
    return all(folded(amount, rows, n) for pieces, order in zip(plans, orders)
        for z in range(line) for pair in sending(z, line, pieces, order) for amount in pair if amount)


def stages(rows):
    return [(0, MOST)] + cuts(MOST, rows, PARTS, ROWS)


def gather_kernel(n, widths, *refs):
    (share_hbm, gain_hbm), ins, (buf, scale_ref, share_ref, gain_ref, first, second, left, right, sums, pairs, early, row_sem, in_sem, sum_sem, early_send, early_recv, send_sem, recv_sem, token) = refs[:2], refs[2:8], refs[8:]
    rows = first.shape[0]
    total = sum(widths)
    line = n // 2
    me = lax.axis_index("shard")
    z, y = me // 2, me % 2
    other = z * 2 + 1 - y
    core = lax.axis_index("width") % 2
    plans = [plan(rows, line, k) for k in range(2)]
    orders = [relays(line, pieces) for pieces in plans]
    up, down, always = z < line - 1, z > 0, z >= 0
    conditions = (up, down, always)
    targets = (jnp.minimum(z + 1, line - 1) * 2 + y, jnp.maximum(z - 1, 0) * 2 + y, other)
    starts = [sum(widths[:i]) for i in range(len(widths))]

    vectors = [
        pltpu.make_async_copy(source, dest, row_sem.at[i])
        for i, (source, dest) in enumerate(((share_hbm, share_ref), (gain_hbm, gain_ref)))
    ]
    for copy in vectors:
        copy.start()
    parts = stages(rows)

    def load(p):
        low, size = parts[p]
        for i, ref in enumerate(ins):
            dest = (first, second)[i % 2].at[pl.ds(low, size), pl.ds(starts[i // 2], widths[i // 2])]
            pltpu.make_async_copy(ref.at[pl.ds(low, size), :], dest, in_sem.at[p, i % 2]).start()

    def loaded(p):
        for i, ref in enumerate((first, second)):
            whole = ref.at[pl.ds(parts[p][0], parts[p][1]), :]
            pltpu.make_async_copy(whole, whole, in_sem.at[p, i]).wait()

    for p in range(FLIGHT):
        load(p)

    barrier = pltpu.get_barrier_semaphore()
    for way, condition in enumerate(conditions):
        @pl.when(condition)
        def _():
            pl.semaphore_signal(barrier, inc=1, device_id={"shard": targets[way]}, device_id_type=MESH)

    for copy in vectors:
        copy.wait()
    for low in range(0, rows, LANES):
        size = min(LANES, rows - low)
        share, gain = share_ref[:, low:low + size], gain_ref[:, low:low + size]
        for ref, row in ((left, share * gain), (right, (1.0 - share) * gain)):
            ref[pl.ds(low, size), :] = jnp.transpose(jnp.broadcast_to(row, (LANES, size)))

    def mixed(block, acc):
        at = pl.ds(pl.multiple_of(block * ROWS, ROWS), ROWS)
        ours, theirs = (jnp.concatenate([ref[at, :]] * 4, axis=1) for ref in (left, right))
        out = []
        for i in range(len(acc)):
            cols = pl.ds(i * 512, 512)
            value = ours * first[at, cols] + theirs * second[at, cols]
            first[at, cols] = value
            square = value * value
            out.append(acc[i] + square[:8] + square[8:])
        return tuple(out)

    def early_copy(way, low, size):
        return pltpu.make_async_remote_copy(
            src_ref=first.at[pl.ds(low, size), :], dst_ref=early.at[way, pl.ds(low, size), :],
            send_sem=early_send.at[way], recv_sem=early_recv.at[way],
            device_id={"shard": targets[way]}, device_id_type=MESH)

    def start_early(level, ways, low, end):
        for way in ways:
            if way in early_from(level, line) and end > low:
                early_copy(way, low, end - low).start()

    def each_level(act):
        for k in range(2):
            for level in range(line):
                @pl.when((z == level) & (core == k))
                def _():
                    act(level, k)

    def wait_token(level, way):
        if ways_from(level, line).count(1 - way):
            pl.semaphore_wait(token.at[way], 1)

    def send_token(level, way):
        if way in ways_from(level, line):
            pl.semaphore_signal(token.at[way], inc=1, device_id={"shard": targets[way]}, device_id_type=MESH)

    def begun(level, k):
        pl.semaphore_wait(barrier, len(ways_from(level, line)))
        start_early(level, (UP, DOWN, ACROSS), 0, table(FIRST[k], level, line))
        if level == line - 1:
            send_token(level, DOWN)

    def risen(level):
        wait_token(level, UP)
        send_token(level, UP)

    acc = tuple(jnp.zeros((8, 512), jnp.float32) for _ in range(total // 512))
    for p, (low, size) in enumerate(parts):
        loaded(p)
        if p + FLIGHT < len(parts):
            load(p + FLIGHT)
        acc = lax.fori_loop(low // ROWS, (low + size) // ROWS, mixed, acc)
        if p == START:
            each_level(begun)
        for level in range(line):
            if p == min(max(2 * level - 1, 0), len(parts) - 1):
                @pl.when(z == level)
                def _():
                    risen(level)
    for i, value in enumerate(acc):
        sums[me, :, pl.ds(i * 512, 512)] = jnp.sum(value, axis=0, keepdims=True)

    def sum_copy(target, ref, k):
        return pltpu.make_async_remote_copy(
            src_ref=ref, dst_ref=ref, send_sem=sum_sem.at[0], recv_sem=sum_sem.at[k],
            device_id={"shard": target}, device_id_type=MESH)

    def exchanged(level, k):
        first_early, last_early = table(FIRST[k], level, line), plans[k][level][0][1]

        def paired():
            sum_copy(other, sums.at[other], 1).wait_recv()
            pairs[level] = sums[level * 2] + sums[level * 2 + 1]

        def lift(above):
            sum_copy(above * 2 + y, pairs.at[level], 2).start()

        for below in range(level):
            for side in (1 - y, y):
                sum_copy(below * 2 + side, sums.at[me], 2).start()
        sum_copy(other, sums.at[me], 1).start()
        start_early(level, (DOWN, ACROSS), first_early, last_early)
        if level == 0:
            paired()
            lift(1)
        wait_token(level, DOWN)
        if level < line - 1:
            send_token(level, DOWN)
        if level > 0:
            paired()
        for above in range(line - 1, max(level, 1) if level == 0 else level, -1):
            lift(above)
        start_early(level, (UP,), first_early, last_early)
        sum_copy(other, sums.at[pl.ds(0, 2 * (line - 1 - level) + level)], 2).wait_recv()
        for above in range(level + 1, line):
            pairs[above] = sums[above * 2] + sums[above * 2 + 1]
        sum_copy(other, sums.at[pl.ds(0, 2 * level + line - level)], 2).wait_send()

    each_level(exchanged)
    whole = pairs[0]
    for level in range(1, line):
        whole = whole + pairs[level]
    scale = jnp.sqrt(whole)
    scale_ref[...] = scale
    inverse = jnp.broadcast_to(1.0 / scale, (8, total))

    def scaled(source, ref):
        def step(block, carry):
            at = pl.ds(pl.multiple_of(block * ROWS, ROWS), ROWS)
            for i in range(total // 512):
                cols = pl.ds(i * 512, 512)
                wide = jnp.concatenate([inverse[:, i * 512:(i + 1) * 512]] * 2, axis=0)
                buf[source, at, cols] = (ref[at, cols] * wide).astype(buf.dtype)
            return carry
        return step

    def copy(way, source, piece, c, own=False):
        low, size = piece
        ref = buf.at[source, pl.ds(low, size), :]
        return pltpu.make_async_remote_copy(
            src_ref=ref, dst_ref=ref, send_sem=send_sem.at[way, 0 if own else 1], recv_sem=recv_sem.at[source, c],
            device_id={"shard": targets[way]}, device_id_type=MESH)

    def rest(level, k):
        pieces, order = plans[k], orders[k]
        leaving, early_ways = ways_from(level, line), early_from(level, line)

        def scale_rows(source, ref, low, size):
            lax.fori_loop(low // ROWS, (low + size) // ROWS, scaled(source, ref), 0)

        def issue_own(c):
            for way in leaving:
                if c or way not in early_ways:
                    copy(way, me, pieces[level][c], c, True).start()

        for c in (1, 0, 2, 3):
            scale_rows(me, first, *pieces[level][c])
            if c != 1:
                issue_own(1 if c == 0 else 0 if c == 2 else 2)
        issue_own(3)

        came = ((level + 1, DOWN, me + 2), (level - 1, UP, me - 2), (level, ACROSS, other))
        for at, slot, source in came:
            if 0 <= at < line and slot in early_from(at, line):
                piece = pieces[at][0]
                early_copy(slot, *piece).wait_recv()
                scale_rows(source, early.at[slot], *piece)

        for column, at, c, ways, direct in order[level]:
            source = at * 2 + (1 - y if column else y)
            if not direct:
                copy(ACROSS, source, pieces[at][c], c).wait_recv()
            for way in ways:
                copy(way, source, pieces[at][c], c).start()
        amounts = sending(level, line, pieces, order)
        for way, relayed in ((way, relayed) for way in leaving for relayed in range(2)):
            amount = amounts[way][relayed]
            if amount:
                depth = folded(amount, rows, n)
                ref = buf.at[pl.ds(0, depth), pl.ds(0, amount // depth), :]
                pltpu.make_async_remote_copy(
                    src_ref=ref, dst_ref=ref, send_sem=send_sem.at[way, relayed], recv_sem=recv_sem.at[0, 0],
                    device_id={"shard": targets[way]}, device_id_type=MESH).wait_send()
        for way in early_ways:
            early_copy(way, *pieces[level][0]).wait_send()

    each_level(rest)


def store_kernel(widths, buf, scale_ref, *refs):
    outs, scales, sem = refs[:3], refs[3:6], refs[6]
    copies = []
    start = 0
    for i, width in enumerate(widths):
        copies.append(pltpu.make_async_copy(buf.at[:, :, pl.ds(start, width)], outs[i], sem.at[0, i]))
        copies.append(pltpu.make_async_copy(scale_ref.at[:, pl.ds(start, width)], scales[i], sem.at[1, i]))
        start += width
    for copy in copies:
        copy.start()
    for copy in copies:
        copy.wait()


def routed(n, one_query, other_query, one_key, other_key, one_value, other_value, mix_share, norm_gain):
    widths = (one_query.shape[1], one_key.shape[1], one_value.shape[1])
    rows, total = one_query.shape[0], sum(widths)
    pieces = len(plan(rows, n // 2, 0)[0])
    vmem = pl.BlockSpec(memory_space=pltpu.VMEM)
    hbm = pl.BlockSpec(memory_space=pl.ANY)
    buf, scale = pl.pallas_call(
        functools.partial(gather_kernel, n, widths),
        out_shape=(pltpu.VMEM((n, rows, total), jnp.bfloat16), pltpu.VMEM((1, total), jnp.float32)),
        in_specs=[hbm] * 8,
        out_specs=(vmem, vmem),
        scratch_shapes=[
            pltpu.VMEM((1, rows), jnp.float32),
            pltpu.VMEM((1, rows), jnp.float32),
            pltpu.VMEM((rows, total), jnp.float32),
            pltpu.VMEM((rows, total), jnp.float32),
            pltpu.VMEM((rows, LANES), jnp.float32),
            pltpu.VMEM((rows, LANES), jnp.float32),
            pltpu.VMEM((n, 1, total), jnp.float32),
            pltpu.VMEM((n // 2, 1, total), jnp.float32),
            pltpu.VMEM((3, MOST, total), jnp.float32),
            pltpu.SemaphoreType.DMA((2,)),
            pltpu.SemaphoreType.DMA((PARTS + 1, 2)),
            pltpu.SemaphoreType.DMA((3,)),
            pltpu.SemaphoreType.DMA((3,)),
            pltpu.SemaphoreType.DMA((3,)),
            pltpu.SemaphoreType.DMA((3, 2)),
            pltpu.SemaphoreType.DMA((n, pieces)),
            pltpu.SemaphoreType.REGULAR((2,)),
        ],
        compiler_params=pltpu.CompilerParams(collective_id=0, has_side_effects=True, vmem_limit_bytes=44 * 2**20),
    )(mix_share[None, :], norm_gain[None, :], one_query, other_query, one_key, other_key, one_value, other_value)
    outs = pl.pallas_call(
        functools.partial(store_kernel, widths),
        out_shape=tuple(jax.ShapeDtypeStruct((n, rows, width), jnp.bfloat16) for width in widths)
        + tuple(jax.ShapeDtypeStruct((1, width), jnp.float32) for width in widths),
        in_specs=[vmem, vmem],
        out_specs=(hbm,) * 6,
        scratch_shapes=[pltpu.SemaphoreType.DMA((2, 3))],
        compiler_params=pltpu.CompilerParams(vmem_limit_bytes=2**20),
    )(pltpu.with_memory_space_constraint(buf, pltpu.VMEM), pltpu.with_memory_space_constraint(scale, pltpu.VMEM))
    return tuple(out.reshape(n * rows, -1) for out in outs[:3]) + tuple(out[0] for out in outs[3:])


def solution(mesh):
    n = mesh.shape["shard"]

    def body(*args):
        return routed(n, *args) if fits(n, args[0].shape[0]) else plain(*args)

    return jax.shard_map(
        body,
        mesh=mesh,
        in_specs=(
            P("shard", "width"),
            P("shard", "width"),
            P("shard", "width"),
            P("shard", "width"),
            P("shard", "width"),
            P("shard", "width"),
            P("shard"),
            P("shard"),
        ),
        out_specs=(
            P(None, "width"),
            P(None, "width"),
            P(None, "width"),
            P("width"),
            P("width"),
            P("width"),
        ),
        check_vma=False,
    )
```

time: 155 us -> 154 us (level)
  no operation moved by 1% of the time
where the time goes in v2:
time: 154 us
  Pallas kernels  154 us (100%)
    pallas_call x1, Pallas kernels, routed(): pl.pallas_call(functools.partial(gather_kernel, n, widths), out_shape=(pl...  148 us
    pallas_call x1, Pallas kernels, routed(): pl.pallas_call(functools.partial(store_kernel, widths), out_shape=tuple((...  5.42 us

profile of v2, /device:TPU:0, one launch (start us, length us, event | category | flops | bytes accessed | tf_op | source)
XLA Modules:
  0.0 154.1 jit_solution(1802198491685953385)
XLA Ops:
  0.6 148.1 %shard_map.127 = (bf16[8,448,2048]{2,1,0:T(8,128)(2,1)S(1)}, f32[1,2048]{1,0:T(1,128)S(1)}) custom-call(f32[1,448]{1,0:T(1,128)} %bitcast.8, f32[1,448]{1,0:T(1,128)} %bitcast.9, f32[448,1024]{1,0:T(8,128)} %refs_2_.1, f32[448,1024]{1,0:T(8,128)} %refs_3_.1, f32[448,512]{1,0:T(8,128)} %refs_4_.1, f32[448,512]{1,0:T(8,128)} %refs_5_.1, f32[448,512]{1,0:T(8,128)} %refs_6_.1, ...), custom_call_target="tpu_custom_call" | custom-call | tf_op jit(solution)/shard_map/pallas_call | solution.py:380
  148.7 5.4 %shard_map.128 = (bf16[8,448,1024]{2,1,0:T(8,128)(2,1)}, bf16[8,448,512]{2,1,0:T(8,128)(2,1)}, bf16[8,448,512]{2,1,0:T(8,128)(2,1)}, f32[1,1024]{1,0:T(1,128)}, f32[1,512]{1,0:T(1,128)}, /*index=5*/f32[1,512]{1,0:T(1,128)}) custom-call(bf16[8,448,2048]{2,1,0:T(8,128)(2,1)S(1)} %get-tuple-element.14.buf, f32[1,2048]{1,0:T(1,128)S(1)} %get-tuple-element.15.scale_ref), custom_call_target="tpu_custom_call" | custom-call | tf_op jit(solution)/shard_map/pallas_call | solution.py:406

commit v3 on v2

--- a/solution.py
+++ b/solution.py
@@ -12,8 +12,8 @@
 ROWS = 16
 TILE = 8
 LANES = 128
-FIRST = ((16, 16, 16, 0), (8, 8, 16, 0))
-LEADS = ((48, 48, 32, 32), (16, 16, 16, 16))
+FIRST = ((16, 16, 16, 0), (16, 16, 16, 0))
+LEADS = ((32, 32, 32, 16), (32, 32, 16, 16))
 UP, DOWN, ACROSS = range(3)
 PARTS = 5
 FLIGHT = 3
@@ -169,14 +169,16 @@
             whole = ref.at[pl.ds(parts[p][0], parts[p][1]), :]
             pltpu.make_async_copy(whole, whole, in_sem.at[p, i]).wait()
 
-    for p in range(FLIGHT):
-        load(p)
+    load(0)
 
     barrier = pltpu.get_barrier_semaphore()
     for way, condition in enumerate(conditions):
         @pl.when(condition)
         def _():
             pl.semaphore_signal(barrier, inc=1, device_id={"shard": targets[way]}, device_id_type=MESH)
+
+    for p in range(1, len(parts)):
+        load(p)
 
     for copy in vectors:
         copy.wait()
@@ -237,8 +239,6 @@
     acc = tuple(jnp.zeros((8, 512), jnp.float32) for _ in range(total // 512))
     for p, (low, size) in enumerate(parts):
         loaded(p)
-        if p + FLIGHT < len(parts):
-            load(p + FLIGHT)
         acc = lax.fori_loop(low // ROWS, (low + size) // ROWS, mixed, acc)
         if p == START:
             each_level(begun)

time: 154 us -> 153 us (level)
  no operation moved by 1% of the time
where the time goes in v3:
time: 153 us
  Pallas kernels  153 us (100%)
    pallas_call x1, Pallas kernels, routed(): pl.pallas_call(functools.partial(gather_kernel, n, widths), out_shape=(pl...  147 us
    pallas_call x1, Pallas kernels, routed(): pl.pallas_call(functools.partial(store_kernel, widths), out_shape=tuple((...  5.42 us

profile of v3, /device:TPU:0, one launch (start us, length us, event | category | flops | bytes accessed | tf_op | source)
XLA Modules:
  0.0 153.3 jit_solution(13365567356792670673)
XLA Ops:
  0.6 147.3 %shard_map.127 = (bf16[8,448,2048]{2,1,0:T(8,128)(2,1)S(1)}, f32[1,2048]{1,0:T(1,128)S(1)}) custom-call(f32[1,448]{1,0:T(1,128)} %bitcast.8, f32[1,448]{1,0:T(1,128)} %bitcast.9, f32[448,1024]{1,0:T(8,128)} %refs_2_.1, f32[448,1024]{1,0:T(8,128)} %refs_3_.1, f32[448,512]{1,0:T(8,128)} %refs_4_.1, f32[448,512]{1,0:T(8,128)} %refs_5_.1, f32[448,512]{1,0:T(8,128)} %refs_6_.1, ...), custom_call_target="tpu_custom_call" | custom-call | tf_op jit(solution)/shard_map/pallas_call | solution.py:380
  147.9 5.4 %shard_map.128 = (bf16[8,448,1024]{2,1,0:T(8,128)(2,1)}, bf16[8,448,512]{2,1,0:T(8,128)(2,1)}, bf16[8,448,512]{2,1,0:T(8,128)(2,1)}, f32[1,1024]{1,0:T(1,128)}, f32[1,512]{1,0:T(1,128)}, /*index=5*/f32[1,512]{1,0:T(1,128)}) custom-call(bf16[8,448,2048]{2,1,0:T(8,128)(2,1)S(1)} %get-tuple-element.14.buf, f32[1,2048]{1,0:T(1,128)S(1)} %get-tuple-element.15.scale_ref), custom_call_target="tpu_custom_call" | custom-call | tf_op jit(solution)/shard_map/pallas_call | solution.py:406

commit v4 on v3

--- a/solution.py
+++ b/solution.py
@@ -19,6 +19,7 @@
 FLIGHT = 3
 MOST = max(map(max, LEADS))
 START = 0
+GAPS = ((0, 0), (2, 1))
 
 
 def plain(one_query, other_query, one_key, other_key, one_value, other_value, mix_share, norm_gain):
@@ -318,16 +319,23 @@
         def scale_rows(source, ref, low, size):
             lax.fori_loop(low // ROWS, (low + size) // ROWS, scaled(source, ref), 0)
 
+        gaps = GAPS[k][level] if level < 2 else 0
+        last = len(pieces[level]) - 1
+        events = [(1, level, last - 1), (1, level, last)][:gaps]
+        held = []
+
         def issue_own(c):
             for way in leaving:
-                if c or way not in early_ways:
+                if c == last and way in early_ways and gaps:
+                    held.append((way, me, pieces[level][c], c, True))
+                elif c or way not in early_ways:
                     copy(way, me, pieces[level][c], c, True).start()
 
         for c in (1, 0, 2, 3):
             scale_rows(me, first, *pieces[level][c])
             if c != 1:
                 issue_own(1 if c == 0 else 0 if c == 2 else 2)
-        issue_own(3)
+        issue_own(last)
 
         came = ((level + 1, DOWN, me + 2), (level - 1, UP, me - 2), (level, ACROSS, other))
         for at, slot, source in came:
@@ -341,7 +349,16 @@
             if not direct:
                 copy(ACROSS, source, pieces[at][c], c).wait_recv()
             for way in ways:
-                copy(way, source, pieces[at][c], c).start()
+                if events and way in early_ways:
+                    held.append((way, source, pieces[at][c], c))
+                else:
+                    copy(way, source, pieces[at][c], c).start()
+            if events and (column, at, c) == events[0]:
+                events.pop(0)
+                ready = 1 if events else len(held)
+                for args in held[:ready]:
+                    copy(*args).start()
+                del held[:ready]
         amounts = sending(level, line, pieces, order)
         for way, relayed in ((way, relayed) for way in leaving for relayed in range(2)):
             amount = amounts[way][relayed]

time: 153 us -> 153 us (level); the launches traced: 153 us -> 151 us
  Pallas kernels: 153 us -> 150 us
    pallas_call x1, Pallas kernels: 147 us -> 145 us  [routed(): pl.pallas_call(functools.partial(gather_kernel, n, widths), out_shape=(pl...]
where the time goes in v4:
time: 153 us; the launch traced here: 151 us
  Pallas kernels  150 us (98%)
    pallas_call x1, Pallas kernels, routed(): pl.pallas_call(functools.partial(gather_kernel, n, widths), out_shape=(pl...  145 us
    pallas_call x1, Pallas kernels, routed(): pl.pallas_call(functools.partial(store_kernel, widths), out_shape=tuple((...  5.42 us

profile of v4, /device:TPU:0, one launch (start us, length us, event | category | flops | bytes accessed | tf_op | source)
XLA Modules:
  0.0 151.0 jit_solution(3191101522947562081)
XLA Ops:
  0.6 144.9 %shard_map.127 = (bf16[8,448,2048]{2,1,0:T(8,128)(2,1)S(1)}, f32[1,2048]{1,0:T(1,128)S(1)}) custom-call(f32[1,448]{1,0:T(1,128)} %bitcast.8, f32[1,448]{1,0:T(1,128)} %bitcast.9, f32[448,1024]{1,0:T(8,128)} %refs_2_.1, f32[448,1024]{1,0:T(8,128)} %refs_3_.1, f32[448,512]{1,0:T(8,128)} %refs_4_.1, f32[448,512]{1,0:T(8,128)} %refs_5_.1, f32[448,512]{1,0:T(8,128)} %refs_6_.1, ...), custom_call_target="tpu_custom_call" | custom-call | tf_op jit(solution)/shard_map/pallas_call | solution.py:397
  145.6 5.4 %shard_map.128 = (bf16[8,448,1024]{2,1,0:T(8,128)(2,1)}, bf16[8,448,512]{2,1,0:T(8,128)(2,1)}, bf16[8,448,512]{2,1,0:T(8,128)(2,1)}, f32[1,1024]{1,0:T(1,128)}, f32[1,512]{1,0:T(1,128)}, /*index=5*/f32[1,512]{1,0:T(1,128)}) custom-call(bf16[8,448,2048]{2,1,0:T(8,128)(2,1)S(1)} %get-tuple-element.14.buf, f32[1,2048]{1,0:T(1,128)S(1)} %get-tuple-element.15.scale_ref), custom_call_target="tpu_custom_call" | custom-call | tf_op jit(solution)/shard_map/pallas_call | solution.py:423

commit v5 on v4

--- a/solution.py
+++ b/solution.py
@@ -16,7 +16,6 @@
 LEADS = ((32, 32, 32, 16), (32, 32, 16, 16))
 UP, DOWN, ACROSS = range(3)
 PARTS = 5
-FLIGHT = 3
 MOST = max(map(max, LEADS))
 START = 0
 GAPS = ((0, 0), (2, 1))
@@ -376,15 +375,17 @@
 
 def store_kernel(widths, buf, scale_ref, *refs):
     outs, scales, sem = refs[:3], refs[3:6], refs[6]
-    copies = []
     start = 0
+    waits = []
     for i, width in enumerate(widths):
-        copies.append(pltpu.make_async_copy(buf.at[:, :, pl.ds(start, width)], outs[i], sem.at[0, i]))
-        copies.append(pltpu.make_async_copy(scale_ref.at[:, pl.ds(start, width)], scales[i], sem.at[1, i]))
+        cols = pl.ds(start, width)
+        for source in range(buf.shape[0]):
+            pltpu.make_async_copy(buf.at[source, :, cols], outs[i].at[source], sem.at[0, i]).start()
+        pltpu.make_async_copy(scale_ref.at[:, cols], scales[i], sem.at[1, i]).start()
+        waits.append(pltpu.make_async_copy(buf.at[:, :, cols], outs[i], sem.at[0, i]))
+        waits.append(pltpu.make_async_copy(scale_ref.at[:, cols], scales[i], sem.at[1, i]))
         start += width
-    for copy in copies:
-        copy.start()
-    for copy in copies:
+    for copy in waits:
         copy.wait()
 
 

time: 153 us -> 153 us (level)
  no operation moved by 1% of the time
where the time goes in v5:
time: 153 us; the launch traced here: 151 us
  Pallas kernels  150 us (98%)
    pallas_call x1, Pallas kernels, routed(): pl.pallas_call(functools.partial(gather_kernel, n, widths), out_shape=(pl...  145 us
    pallas_call x1, Pallas kernels, routed(): pl.pallas_call(functools.partial(store_kernel, widths), out_shape=tuple((...  5.24 us

profile of v5, /device:TPU:0, one launch (start us, length us, event | category | flops | bytes accessed | tf_op | source)
XLA Modules:
  0.0 150.8 jit_solution(8810974547946955743)
XLA Ops:
  0.6 144.9 %shard_map.127 = (bf16[8,448,2048]{2,1,0:T(8,128)(2,1)S(1)}, f32[1,2048]{1,0:T(1,128)S(1)}) custom-call(f32[1,448]{1,0:T(1,128)} %bitcast.8, f32[1,448]{1,0:T(1,128)} %bitcast.9, f32[448,1024]{1,0:T(8,128)} %refs_2_.1, f32[448,1024]{1,0:T(8,128)} %refs_3_.1, f32[448,512]{1,0:T(8,128)} %refs_4_.1, f32[448,512]{1,0:T(8,128)} %refs_5_.1, f32[448,512]{1,0:T(8,128)} %refs_6_.1, ...), custom_call_target="tpu_custom_call" | custom-call | tf_op jit(solution)/shard_map/pallas_call | solution.py:398
  145.6 5.2 %shard_map.128 = (bf16[8,448,1024]{2,1,0:T(8,128)(2,1)}, bf16[8,448,512]{2,1,0:T(8,128)(2,1)}, bf16[8,448,512]{2,1,0:T(8,128)(2,1)}, f32[1,1024]{1,0:T(1,128)}, f32[1,512]{1,0:T(1,128)}, /*index=5*/f32[1,512]{1,0:T(1,128)}) custom-call(bf16[8,448,2048]{2,1,0:T(8,128)(2,1)S(1)} %get-tuple-element.14.buf, f32[1,2048]{1,0:T(1,128)S(1)} %get-tuple-element.15.scale_ref), custom_call_target="tpu_custom_call" | custom-call | tf_op jit(solution)/shard_map/pallas_call | solution.py:424

commit v6 on v5

--- a/solution.py
+++ b/solution.py
@@ -64,7 +64,7 @@
 def plan(rows, line, core):
     half = rows // 2 // ROWS * ROWS
     leads = [table(LEADS[core], z, line) for z in range(line)]
-    return [[(0, lead)] + cuts(lead, half, 2, ROWS) + [(half, rows - half)] for lead in leads]
+    return [[(0, lead), (lead, 3 * ROWS), (lead + 3 * ROWS, half - lead - 3 * ROWS), (half, rows - half)] for lead in leads]
 
 
 def ways_from(z, line):
@@ -135,8 +135,9 @@
 
 
 def gather_kernel(n, widths, *refs):
-    (share_hbm, gain_hbm), ins, (buf, scale_ref, share_ref, gain_ref, first, second, left, right, sums, pairs, early, row_sem, in_sem, sum_sem, early_send, early_recv, send_sem, recv_sem, token) = refs[:2], refs[2:8], refs[8:]
-    rows = first.shape[0]
+    (share_hbm, gain_hbm), ins, (buf, scale_ref, share_ref, gain_ref, both, left, right, sums, pairs, early, row_sem, in_sem, sum_sem, early_send, early_recv, send_sem, recv_sem, token) = refs[:2], refs[2:8], refs[8:]
+    first, second = both.at[0], both.at[1]
+    rows = both.shape[1]
     total = sum(widths)
     line = n // 2
     me = lax.axis_index("shard")
@@ -162,12 +163,11 @@
         low, size = parts[p]
         for i, ref in enumerate(ins):
             dest = (first, second)[i % 2].at[pl.ds(low, size), pl.ds(starts[i // 2], widths[i // 2])]
-            pltpu.make_async_copy(ref.at[pl.ds(low, size), :], dest, in_sem.at[p, i % 2]).start()
+            pltpu.make_async_copy(ref.at[pl.ds(low, size), :], dest, in_sem.at[p]).start()
 
     def loaded(p):
-        for i, ref in enumerate((first, second)):
-            whole = ref.at[pl.ds(parts[p][0], parts[p][1]), :]
-            pltpu.make_async_copy(whole, whole, in_sem.at[p, i]).wait()
+        whole = both.at[:, pl.ds(parts[p][0], parts[p][1]), :]
+        pltpu.make_async_copy(whole, whole, in_sem.at[p]).wait()
 
     load(0)
 
@@ -403,15 +403,14 @@
         scratch_shapes=[
             pltpu.VMEM((1, rows), jnp.float32),
             pltpu.VMEM((1, rows), jnp.float32),
-            pltpu.VMEM((rows, total), jnp.float32),
-            pltpu.VMEM((rows, total), jnp.float32),
+            pltpu.VMEM((2, rows, total), jnp.float32),
             pltpu.VMEM((rows, LANES), jnp.float32),
             pltpu.VMEM((rows, LANES), jnp.float32),
             pltpu.VMEM((n, 1, total), jnp.float32),
             pltpu.VMEM((n // 2, 1, total), jnp.float32),
             pltpu.VMEM((3, MOST, total), jnp.float32),
             pltpu.SemaphoreType.DMA((2,)),
-            pltpu.SemaphoreType.DMA((PARTS + 1, 2)),
+            pltpu.SemaphoreType.DMA((PARTS + 1,)),
             pltpu.SemaphoreType.DMA((3,)),
             pltpu.SemaphoreType.DMA((3,)),
             pltpu.SemaphoreType.DMA((3,)),

time: 153 us -> 153 us (level)
  no operation moved by 1% of the time
where the time goes in v6:
time: 153 us; the launch traced here: 151 us
  Pallas kernels  150 us (98%)
    pallas_call x1, Pallas kernels, routed(): pl.pallas_call(functools.partial(gather_kernel, n, widths), out_shape=(pl...  145 us
    pallas_call x1, Pallas kernels, routed(): pl.pallas_call(functools.partial(store_kernel, widths), out_shape=tuple((...  5.24 us

profile of v6, /device:TPU:0, one launch (start us, length us, event | category | flops | bytes accessed | tf_op | source)
XLA Modules:
  0.0 150.7 jit_solution(10224845981675617903)
XLA Ops:
  0.6 144.8 %shard_map.127 = (bf16[8,448,2048]{2,1,0:T(8,128)(2,1)S(1)}, f32[1,2048]{1,0:T(1,128)S(1)}) custom-call(f32[1,448]{1,0:T(1,128)} %bitcast.8, f32[1,448]{1,0:T(1,128)} %bitcast.9, f32[448,1024]{1,0:T(8,128)} %refs_2_.1, f32[448,1024]{1,0:T(8,128)} %refs_3_.1, f32[448,512]{1,0:T(8,128)} %refs_4_.1, f32[448,512]{1,0:T(8,128)} %refs_5_.1, f32[448,512]{1,0:T(8,128)} %refs_6_.1, ...), custom_call_target="tpu_custom_call" | custom-call | tf_op jit(solution)/shard_map/pallas_call | solution.py:398
  145.5 5.2 %shard_map.128 = (bf16[8,448,1024]{2,1,0:T(8,128)(2,1)}, bf16[8,448,512]{2,1,0:T(8,128)(2,1)}, bf16[8,448,512]{2,1,0:T(8,128)(2,1)}, f32[1,1024]{1,0:T(1,128)}, f32[1,512]{1,0:T(1,128)}, /*index=5*/f32[1,512]{1,0:T(1,128)}) custom-call(bf16[8,448,2048]{2,1,0:T(8,128)(2,1)S(1)} %get-tuple-element.14.buf, f32[1,2048]{1,0:T(1,128)S(1)} %get-tuple-element.15.scale_ref), custom_call_target="tpu_custom_call" | custom-call | tf_op jit(solution)/shard_map/pallas_call | solution.py:423
